TPU v7x, 32 devices: a whole 2x2x4 slice. The times are simulated.
32 devices in a mesh: groups: 2 (over y), rows: 4 (over z), cols: 2 (over x), sub: 2 (over core).
Axes of the slice: x: 2, y: 2, z: 4, core: 2. Of those that a mesh axis runs over, the one named last changes fastest.
Arguments:
- diagonal_tiles: float32 [256, 128, 128], P(('groups', 'rows', 'sub')), parts along dimension 0
- coupling_tiles: float32 [256, 6, 128, 128], P(('groups', 'rows', 'sub'), 'cols'), parts along dimension 0, may hold values from -0.0625 to 0.0625
- column_part: int32 [256, 6], P(('groups', 'rows', 'sub'), 'cols'), parts along dimension 0, may hold values from 0 to 4
- column_tile: int32 [256, 6], P(('groups', 'rows', 'sub'), 'cols'), parts along dimension 0, may hold values from 0 to 31
- neighbours: int32 [8, 4], P('groups'), parts along dimension 0, may hold values from 0 to 3, as said below
- right_side: float32 [256, 128], P(('groups', 'rows', 'sub')), parts along dimension 0, may hold values from -6 to 6
- jacobi_inverse: float32 [256, 128, 128], P(('groups', 'rows', 'sub')), parts along dimension 0, as said below
Outputs:
- solution: float32 [256, 128], P(('groups', 'rows', 'sub')), parts along dimension 0
- residual: float32 [256, 128], P(('groups', 'rows', 'sub')), parts along dimension 0
There are 2 independent parts, one for each index of `groups`. A program takes and returns all parts, laid end to end along the dimension named above; each array names one. Nothing has to cross between parts.
Inputs may be any that keep to these rules, and one draw needn't show every extreme that they name: `neighbours`: entry 0 of partition p's list is (p + 4 // 2) mod 4, the opposite partition on the cycle; every other entry names a partition whose index differs from p by 1 to 2 (without wrapping round); entries may repeat. `jacobi_inverse`: block-diagonal: each group of 5 consecutive variables, from the first on, forms one 5 x 5 block, and each variable left over after the last whole group of 5 is a 1 x 1 block of its own.
All inputs are finite; a program needn't handle non-finite values.
Results may differ from a plain program's by a relative error of at most 0.00019.
Values sent between devices are 32-bit elements; how exact they have to be, the bound alone decides.
A program may use at most 64 MiB of HBM per device.

v0:
```python
import functools

import jax
import jax.numpy as jnp
from jax import lax
from jax.experimental import pallas as pl
from jax.experimental.pallas import tpu as pltpu
from jax.sharding import PartitionSpec as P

MESH = pl.DeviceIdType.MESH
REACH = 2
APPLIES = 4
SUBLANES = 8
F32 = jnp.float32


def offsets_of(count):
    wanted = {d % count for d in range(-REACH, REACH + 1)} | {count // 2}
    return sorted(wanted)


def kernel(
    sizes,
    diag_hbm,
    coup_hbm,
    jac_hbm,
    part_ref,
    tile_ref,
    near_ref,
    right_ref,
    out_ref,
    diag,
    coup,
    jac,
    one_hot,
    prod,
    dprod,
    vec,
    landed,
    recv,
    dots,
    dots_recv,
    load_sem,
    send_sem,
    recv_sem,
    dots_send_sem,
    dots_recv_sem,
):
    n_rows, n_cols, n_sub = sizes
    offsets = offsets_of(n_rows)
    slots = len(offsets)
    rows_dev, slot_count, width, _ = coup.shape
    half_rows = slots * rows_dev
    chunk = rows_dev * SUBLANES
    row = lax.axis_index("rows")
    col = lax.axis_index("cols")
    sub = lax.axis_index("sub")
    me = row * n_sub + sub

    loads = [
        pltpu.make_async_copy(jac_hbm, jac, load_sem.at[0]),
        pltpu.make_async_copy(diag_hbm, diag, load_sem.at[1]),
        pltpu.make_async_copy(coup_hbm, coup, load_sem.at[2]),
    ]
    for load in loads:
        load.start()

    def partner(slot):
        return lax.rem(row + offsets[slot], n_rows)

    def if_linked(slot, act):
        if offsets[slot] in (0, n_rows // 2):
            act()
        else:
            pl.when(jnp.abs(partner(slot) - row) <= REACH)(act)

    def corner(slot, step):
        return {
            "rows": partner(slot),
            "cols": lax.rem(col + step // n_sub, n_cols),
            "sub": lax.rem(sub + step % n_sub, n_sub),
        }

    barrier = pltpu.get_barrier_semaphore()

    def dot_peers():
        for step in range(1, n_rows * n_sub):
            peer = lax.rem(me + step, n_rows * n_sub)
            yield step, peer, {"rows": lax.div(peer, n_sub), "cols": col, "sub": lax.rem(peer, n_sub)}

    recv[...] = jnp.zeros_like(recv)
    for _, _, where in dot_peers():
        pl.semaphore_signal(barrier, inc=1, device_id=where, device_id_type=MESH)
    for slot in range(slots):
        for step in range(n_sub, n_cols * n_sub):

            def greet(slot=slot, step=step):
                where = corner(slot, step)
                pl.semaphore_signal(barrier, inc=1, device_id=where, device_id_type=MESH)

            if_linked(slot, greet)

    part = part_ref[...]
    tile = tile_ref[...]
    target = jnp.full(part.shape, row, jnp.int32)
    for j in range(near_ref.shape[1]):
        target = jnp.where(part == j + 1, near_ref[row, j], target)
    apart = target - row
    apart = jnp.where(apart < 0, apart + n_rows, apart)
    place = jnp.zeros(part.shape, jnp.int32)
    for slot in range(1, slots):
        place = jnp.where(apart == offsets[slot], slot, place)
    landing = place * rows_dev + tile
    for j in range(1, n_sub):
        landing = jnp.where(tile >= j * rows_dev, landing + (half_rows - rows_dev), landing)
    from_row = lax.broadcasted_iota(jnp.int32, (rows_dev, chunk), 0)
    to_lane = lax.broadcasted_iota(jnp.int32, (rows_dev, chunk), 1)
    first = from_row * SUBLANES
    spread = ((to_lane >= first) & (to_lane < first + SUBLANES)).astype(F32)
    spread_landing = jnp.dot(
        landing.astype(F32), spread, precision=lax.Precision.HIGHEST, preferred_element_type=F32
    )
    at_row = lax.broadcasted_iota(jnp.int32, (n_sub * half_rows, chunk), 0).astype(F32)
    for k in range(slot_count):
        hit = (spread_landing[k : k + 1] == at_row).astype(F32)
        one_hot[:, k * chunk : (k + 1) * chunk] = hit.astype(jnp.bfloat16)

    loads[0].wait()

    def turn(r, carry):
        jac[r] = jnp.transpose(jac[r])
        return carry

    lax.fori_loop(0, rows_dev, turn, 0, unroll=4)

    def block(e, slot, to_sub):
        at = pl.multiple_of(to_sub * half_rows + slot * rows_dev, rows_dev)
        return landed.at[e, pl.ds(at, rows_dev)]

    def owner_copy(e, slot, step):
        back = offsets.index(-offsets[slot] % n_rows)
        where = corner(slot, step)
        return pltpu.make_async_remote_copy(
            src_ref=block(e, slot, where["sub"]),
            dst_ref=recv.at[e, back, col, sub],
            send_sem=send_sem.at[e, slot, step],
            recv_sem=recv_sem.at[e, back, col, sub],
            device_id=where,
            device_id_type=MESH,
        )

    def owner_arrival(e, slot, step):
        where = corner(slot, step)
        return pltpu.make_async_remote_copy(
            src_ref=block(e, slot, where["sub"]),
            dst_ref=recv.at[e, slot, where["cols"], where["sub"]],
            send_sem=send_sem.at[e, slot, step],
            recv_sem=recv_sem.at[e, slot, where["cols"], where["sub"]],
            device_id=where,
            device_id_type=MESH,
        )

    far_first = sorted(range(slots), key=lambda s: -min(offsets[s], n_rows - offsets[s]))
    routes = [(s, c) for s in far_first for c in reversed(range(n_cols * n_sub)) if (s, c) != (0, 0)]

    def each_route(act):
        for slot, step in routes:
            if_linked(slot, functools.partial(act, slot, step))

    def dots_copy(e, step, peer, where):
        return pltpu.make_async_remote_copy(
            src_ref=dots.at[e],
            dst_ref=dots_recv.at[e, pl.ds(me, 1)],
            send_sem=dots_send_sem.at[e, step],
            recv_sem=dots_recv_sem.at[e, me],
            device_id=where,
            device_id_type=MESH,
        )

    def dots_start(e, products):
        at = lax.broadcasted_iota(jnp.int32, (1, width), 1)
        line = jnp.zeros((1, width), F32)
        for j, product in enumerate(products):
            total = jnp.sum(jnp.sum(product, axis=0, keepdims=True), axis=1, keepdims=True)
            line = jnp.where(at == j, total, line)
        dots[e] = line
        for step, peer, where in dot_peers():
            dots_copy(e, step, peer, where).start()
        dots_recv[e, pl.ds(me, 1)] = line

    def dots_finish(e, count):
        for step, peer, where in dot_peers():
            pltpu.make_async_remote_copy(
                src_ref=dots.at[e],
                dst_ref=dots_recv.at[e, pl.ds(peer, 1)],
                send_sem=dots_send_sem.at[e, step],
                recv_sem=dots_recv_sem.at[e, peer],
                device_id=where,
                device_id_type=MESH,
            ).wait_recv()
        total = jnp.sum(dots_recv[e], axis=0, keepdims=True)
        return [jnp.broadcast_to(total[:, j : j + 1], total.shape) for j in range(count)]

    def fold(product):
        return jnp.sum(product.reshape(width // SUBLANES, SUBLANES, width), axis=0)

    unroll = 8 if rows_dev % 8 == 0 else 1

    def apply(e, value):
        vec[e] = value
        if e == 0:
            loads[1].wait()
            loads[2].wait()

        def some_rows(g, carry):
            for u in range(unroll):
                r = g * unroll + u
                hat = jnp.sum(jac[r] * vec[e, pl.ds(r, 1)], axis=1, keepdims=True)
                hat = jnp.broadcast_to(hat, (width, width))
                for k in range(slot_count):
                    at = pl.multiple_of(k * chunk + r * SUBLANES, SUBLANES)
                    prod[pl.ds(at, SUBLANES)] = fold(coup[r, k] * hat)
                dprod[pl.ds(pl.multiple_of(r * SUBLANES, SUBLANES), SUBLANES)] = fold(diag[r] * hat)
            return carry

        lax.fori_loop(0, rows_dev // unroll, some_rows, 0)
        rest = prod[...]
        out = None
        for _ in range(3):
            piece = rest.astype(jnp.bfloat16)
            rest = rest - piece.astype(F32)
            term = jnp.dot(one_hot[...], piece, preferred_element_type=F32)
            out = term if out is None else out + term
        landed[e] = out
        if e == 0:
            greetings = n_rows * n_sub - 1
            for slot in range(slots):
                linked = 1
                if offsets[slot] not in (0, n_rows // 2):
                    linked = (jnp.abs(partner(slot) - row) <= REACH).astype(jnp.int32)
                greetings = greetings + (n_cols - 1) * n_sub * linked
            pl.semaphore_wait(barrier, greetings)
        each_route(lambda slot, step: owner_copy(e, slot, step).start())
        recv[e, 0, col, sub] = landed[e, pl.ds(pl.multiple_of(sub * half_rows, rows_dev), rows_dev)]
        own = jnp.sum(dprod[...].reshape(rows_dev, SUBLANES, width), axis=1)
        each_route(lambda slot, step: owner_arrival(e, slot, step).wait_recv())
        for slot in range(slots):
            for c in range(n_cols):
                for s in range(n_sub):
                    own = own + recv[e, slot, c, s]
        return own

    shadow = right_ref[...]
    image = apply(0, shadow)
    dots_start(0, [shadow * shadow, shadow * image])
    second = apply(1, image)
    rho, shadow_image = dots_finish(0, 2)
    alpha = rho / shadow_image
    half = shadow - alpha * image
    twice = image - alpha * second
    dots_start(1, [twice * half, twice * twice, shadow * half, shadow * twice])
    third = apply(2, twice)
    cross, square, shadow_half, shadow_twice = dots_finish(1, 4)
    omega = cross / square
    rho_next = shadow_half - omega * shadow_twice
    beta = rho_next / rho * (alpha / omega)
    residual = half - omega * twice
    search = residual + beta * (shadow - omega * image)
    residual_image = twice - omega * third
    image = residual_image + beta * (image - omega * second)
    dots_start(2, [shadow * image])
    fourth = apply(3, image)
    alpha_next = rho_next / dots_finish(2, 1)[0]
    half_next = residual - alpha_next * image
    twice = residual_image - alpha_next * fourth
    dots_start(3, [twice * half_next, twice * twice])

    vec[0] = alpha * shadow + omega * half + alpha_next * search
    vec[1] = half_next
    at_lane = lax.broadcasted_iota(jnp.int32, (width, width), 1)

    def hats(r, carry):
        for j in range(2):
            hat = jnp.sum(jac[r] * vec[j, pl.ds(r, 1)], axis=1, keepdims=True)
            carry = jnp.where(at_lane == j * rows_dev + r, hat, carry)
        return carry

    hat = lax.fori_loop(0, rows_dev, hats, jnp.zeros((width, width), F32), unroll=4)
    hat = jnp.transpose(hat)
    cross, square = dots_finish(3, 2)
    omega = cross / square
    out_ref[:rows_dev] = hat[:rows_dev] + omega * hat[rows_dev : 2 * rows_dev]
    out_ref[rows_dev:] = half_next - omega * twice

    for e in range(APPLIES):
        each_route(lambda slot, step: owner_copy(e, slot, step).wait_send())
        for step, peer, where in dot_peers():
            dots_copy(e, step, peer, where).wait_send()


def split(both_ref, sol_ref, res_ref):
    rows_dev = sol_ref.shape[0]
    sol_ref[...] = both_ref[:rows_dev]
    res_ref[...] = both_ref[rows_dev:]


def on_device(
    diagonal_tiles, coupling_tiles, column_part, column_tile, neighbours, right_side, jacobi_inverse
):
    n_rows, n_cols, n_sub = (lax.axis_size(a) for a in ("rows", "cols", "sub"))
    slots = len(offsets_of(n_rows))
    rows_dev, slot_count, width, _ = coupling_tiles.shape
    half_rows = slots * rows_dev
    chunk = rows_dev * SUBLANES
    peers = n_rows * n_sub
    hbm = pl.BlockSpec(memory_space=pl.ANY)
    vmem = pl.BlockSpec(memory_space=pltpu.VMEM)
    dma = pltpu.SemaphoreType.DMA
    scratch = [
        pltpu.VMEM(diagonal_tiles.shape, F32),
        pltpu.VMEM(coupling_tiles.shape, F32),
        pltpu.VMEM(jacobi_inverse.shape, F32),
        pltpu.VMEM((n_sub * half_rows, slot_count * chunk), jnp.bfloat16),
        pltpu.VMEM((slot_count * chunk, width), F32),
        pltpu.VMEM((chunk, width), F32),
        pltpu.VMEM((APPLIES, rows_dev, width), F32),
        pltpu.VMEM((APPLIES, n_sub * half_rows, width), F32),
        pltpu.VMEM((APPLIES, slots, n_cols, n_sub, rows_dev, width), F32),
        pltpu.VMEM((APPLIES, 1, width), F32),
        pltpu.VMEM((APPLIES, peers, width), F32),
        dma((3,)),
        dma((APPLIES, slots, n_cols * n_sub)),
        dma((APPLIES, slots, n_cols, n_sub)),
        dma((APPLIES, peers)),
        dma((APPLIES, peers)),
    ]
    both = pl.pallas_call(
        functools.partial(kernel, (n_rows, n_cols, n_sub)),
        out_shape=jax.ShapeDtypeStruct((2 * rows_dev, width), F32),
        in_specs=[hbm, hbm, hbm, vmem, vmem, pl.BlockSpec(memory_space=pltpu.SMEM), vmem],
        out_specs=vmem,
        scratch_shapes=scratch,
        compiler_params=pltpu.CompilerParams(
            collective_id=0, has_side_effects=True, vmem_limit_bytes=56 * 2**20
        ),
        name="solve",
    )(
        diagonal_tiles,
        coupling_tiles,
        jacobi_inverse,
        column_part.T,
        column_tile.T,
        neighbours,
        right_side,
    )
    out = jax.ShapeDtypeStruct(right_side.shape, F32)
    return pl.pallas_call(
        split, out_shape=(out, out), in_specs=[vmem], out_specs=(vmem, vmem), name="split"
    )(both)


def solution(mesh):
    in_specs = (
        P(("groups", "rows", "sub"), None, None),
        P(("groups", "rows", "sub"), "cols", None, None),
        P(("groups", "rows", "sub"), "cols"),
        P(("groups", "rows", "sub"), "cols"),
        P("groups", None),
        P(("groups", "rows", "sub"), None),
        P(("groups", "rows", "sub"), None, None),
    )
    out_specs = (P(("groups", "rows", "sub"), None), P(("groups", "rows", "sub"), None))
    return jax.shard_map(
        on_device, mesh=mesh, in_specs=in_specs, out_specs=out_specs, check_vma=False
    )
```

profile of v0, /device:TPU:0, one launch (start us, length us, event | category | flops | bytes accessed | tf_op | source)
XLA Modules:
  0.0 34.2 jit_solution(7243270526621961927)
XLA Ops:
  0.6 32.3 %solve.1.both_ref = f32[32,128]{1,0:T(8,128)} custom-call(f32[16,128,128]{2,1,0:T(8,128)} %diag_hbm.1, f32[16,3,128,128]{3,2,1,0:T(8,128)} %coup_hbm.1, f32[16,128,128]{2,1,0:T(8,128)} %jac_hbm.1, s32[3,16]{1,0:T(4,128)} %bitcast.2, s32[3,16]{1,0:T(4,128)} %bitcast.3, s32[4,4]{1,0:T(4,128)} %near_ref.1, f32[16,128]{1,0:T(8,128)} %right_ref.1), custom_call_target="tpu_custom_call" | custom-call | tf_op jit(solution)/shard_map/solve/pallas_call | solution.py:337
  32.9 1.3 %split.1 = (f32[16,128]{1,0:T(8,128)}, f32[16,128]{1,0:T(8,128)}) custom-call(f32[32,128]{1,0:T(8,128)} %solve.1.both_ref), custom_call_target="tpu_custom_call" | custom-call | tf_op jit(solution)/shard_map/split/pallas_call | solution.py:357
where the time goes:
time: 34.5 us; the launch traced here: 34.2 us
  Pallas kernels  33.6 us (97%)
  between operations  0.64 us (2%)
    pallas_call x1, Pallas kernels, on_device(): pl.pallas_call(functools.partial(kernel, (n_rows, n_cols, n_sub)), out_sh...  32.3 us
    pallas_call x1, Pallas kernels, on_device(): pl.pallas_call(split, out_shape=(out, out), in_specs=[vmem], out_specs=(v...  1.32 us

commit v1 on v0

v1 whole, which is shorter than its diff:
```python
import functools

import jax
import jax.numpy as jnp
from jax import lax
from jax.experimental import pallas as pl
from jax.experimental.pallas import tpu as pltpu
from jax.sharding import PartitionSpec as P

MESH = pl.DeviceIdType.MESH
REACH = 2
APPLIES = 4
SUBLANES = 8
MOST_DOTS = 4
F32 = jnp.float32


def offsets_of(count):
    wanted = {d % count for d in range(-REACH, REACH + 1)} | {count // 2}
    return sorted(wanted)


def pieces_of(rows):
    return 8 if rows % 8 == 0 else 1


def kernel(
    sizes,
    diag_hbm,
    coup_hbm,
    jac_hbm,
    part_hbm,
    tile_hbm,
    near_hbm,
    right_hbm,
    out_ref,
    diag,
    coup,
    jac,
    part_ref,
    tile_ref,
    near_ref,
    right_ref,
    one_hot,
    prod,
    dprod,
    vec,
    landed,
    recv,
    dots,
    dots_recv,
    load_sem,
    send_sem,
    recv_sem,
    dots_send_sem,
    dots_recv_sem,
):
    n_rows, n_cols, n_sub = sizes
    offsets = offsets_of(n_rows)
    slots = len(offsets)
    rows_dev, slot_count, width, _ = coup.shape
    half_rows = slots * rows_dev
    chunk = rows_dev * SUBLANES
    peers = n_rows * n_sub
    unroll = pieces_of(rows_dev)
    row = lax.axis_index("rows")
    col = lax.axis_index("cols")
    sub = lax.axis_index("sub")
    me = row * n_sub + sub

    def piece_loads(g):
        at = pl.ds(g * unroll, unroll)
        return [
            pltpu.make_async_copy(diag_hbm.at[at], diag.at[at], load_sem.at[5 + 2 * g]),
            pltpu.make_async_copy(coup_hbm.at[at], coup.at[at], load_sem.at[6 + 2 * g]),
        ]

    small = [
        pltpu.make_async_copy(part_hbm, part_ref, load_sem.at[0]),
        pltpu.make_async_copy(tile_hbm, tile_ref, load_sem.at[1]),
        pltpu.make_async_copy(near_hbm, near_ref, load_sem.at[2]),
        pltpu.make_async_copy(right_hbm, right_ref, load_sem.at[3]),
    ]
    jac_load = pltpu.make_async_copy(jac_hbm, jac, load_sem.at[4])
    for load in small:
        load.start()
    jac_load.start()
    for g in range(rows_dev // unroll):
        for load in piece_loads(g):
            load.start()

    def partner(slot):
        return lax.rem(row + offsets[slot], n_rows)

    def always(slot):
        return offsets[slot] in (0, n_rows // 2)

    def is_linked(slot):
        return jnp.abs(partner(slot) - row) <= REACH

    def if_linked(slot, act):
        if always(slot):
            act()
        else:
            pl.when(is_linked(slot))(act)

    maybe = [slot for slot in range(slots) if not always(slot)]
    linked_count = slots - len(maybe)
    for slot in maybe:
        linked_count = linked_count + is_linked(slot).astype(jnp.int32)

    def for_linked_count(act):
        if not maybe:
            act(slots)
        for total in range(slots - len(maybe), slots + 1) if maybe else ():
            pl.when(linked_count == total)(functools.partial(act, total))

    def corner(slot, step):
        return {
            "rows": partner(slot),
            "cols": lax.rem(col + step // n_sub, n_cols),
            "sub": lax.rem(sub + step % n_sub, n_sub),
        }

    barrier = pltpu.get_barrier_semaphore()

    def dot_peers():
        for step in range(1, peers):
            peer = lax.rem(me + step, peers)
            yield peer, {"rows": lax.div(peer, n_sub), "cols": col, "sub": lax.rem(peer, n_sub)}

    def from_block(slot, c, s):
        return ((slot * n_cols + c) * n_sub + s) * rows_dev

    per_slot = n_cols * n_sub * rows_dev
    for slot in maybe:
        at = pl.ds(slot * per_slot, per_slot)
        for e in range(APPLIES):
            recv[e, at] = jnp.zeros((per_slot, width), F32)

    far_first = sorted(range(slots), key=lambda s: -min(offsets[s], n_rows - offsets[s]))
    for slot in far_first:
        for step in range(n_sub, n_cols * n_sub):

            def greet(slot=slot, step=step):
                where = corner(slot, step)
                pl.semaphore_signal(barrier, inc=1, device_id=where, device_id_type=MESH)

            if_linked(slot, greet)
    for _, where in dot_peers():
        pl.semaphore_signal(barrier, inc=1, device_id=where, device_id_type=MESH)

    for load in small:
        load.wait()
    part = part_ref[...]
    tile = tile_ref[...]
    target = jnp.full(part.shape, row, jnp.int32)
    for j in range(near_ref.shape[1]):
        target = jnp.where(part == j + 1, near_ref[row, j], target)
    apart = target - row
    apart = jnp.where(apart < 0, apart + n_rows, apart)
    place = jnp.zeros(part.shape, jnp.int32)
    for slot in range(1, slots):
        place = jnp.where(apart == offsets[slot], slot, place)
    landing = place * rows_dev + tile
    for j in range(1, n_sub):
        landing = jnp.where(tile >= j * rows_dev, landing + (half_rows - rows_dev), landing)
    from_row = lax.broadcasted_iota(jnp.int32, (rows_dev, chunk), 0)
    to_lane = lax.broadcasted_iota(jnp.int32, (rows_dev, chunk), 1)
    first = from_row * SUBLANES
    spread = ((to_lane >= first) & (to_lane < first + SUBLANES)).astype(F32)
    spread_landing = jnp.dot(
        landing.astype(F32), spread, precision=lax.Precision.HIGHEST, preferred_element_type=F32
    )
    at_row = lax.broadcasted_iota(jnp.int32, (n_sub * half_rows, chunk), 0).astype(F32)
    for k in range(slot_count):
        hit = (spread_landing[k : k + 1] == at_row).astype(F32)
        one_hot[:, k * chunk : (k + 1) * chunk] = hit.astype(jnp.bfloat16)

    jac_load.wait()

    def turn(r, carry):
        jac[r] = jnp.transpose(jac[r])
        return carry

    lax.fori_loop(0, rows_dev, turn, 0, unroll=4)

    def owner_copy(e, slot, step):
        back = offsets.index(-offsets[slot] % n_rows)
        where = corner(slot, step)
        at = pl.multiple_of(where["sub"] * half_rows + slot * rows_dev, rows_dev)
        to = pl.multiple_of(from_block(back, col, sub), rows_dev)
        return pltpu.make_async_remote_copy(
            src_ref=landed.at[e, pl.ds(at, rows_dev)],
            dst_ref=recv.at[e, pl.ds(to, rows_dev)],
            send_sem=send_sem.at[e],
            recv_sem=recv_sem.at[e],
            device_id=where,
            device_id_type=MESH,
        )

    routes = [(s, c) for s in far_first for c in reversed(range(n_cols * n_sub)) if (s, c) != (0, 0)]

    def each_route(act):
        for slot, step in routes:
            if_linked(slot, functools.partial(act, slot, step))

    def await_rows(sem, count):
        some = recv.at[0, pl.ds(0, count)]
        pltpu.make_async_copy(some, some, sem).wait()

    def await_blocks(sem):
        for_linked_count(lambda total: await_rows(sem, total * per_slot - rows_dev))

    def dots_copy(e, count, where):
        return pltpu.make_async_remote_copy(
            src_ref=dots.at[e, pl.ds(0, count)],
            dst_ref=dots_recv.at[e, me, pl.ds(0, count)],
            send_sem=dots_send_sem.at[e],
            recv_sem=dots_recv_sem.at[e],
            device_id=where,
            device_id_type=MESH,
        )

    def dots_start(e, products):
        count = len(products)
        lines = [jnp.sum(product, axis=0, keepdims=True) for product in products]
        for j, line in enumerate(lines):
            dots[e, j : j + 1] = line
        for _, where in dot_peers():
            dots_copy(e, count, where).start()
        for j, line in enumerate(lines):
            dots_recv[e, me, j : j + 1] = line

    def dots_finish(e, count):
        await_rows(dots_recv_sem.at[e], (peers - 1) * count)
        lines = jnp.sum(dots_recv[e, :, :count], axis=0)
        total = jnp.sum(lines, axis=1, keepdims=True)
        return [jnp.broadcast_to(total[j : j + 1], (1, width)) for j in range(count)]

    def fold(product):
        return jnp.sum(product.reshape(width // SUBLANES, SUBLANES, width), axis=0)

    def send_products(e, value):
        if e > 0:
            vec[e] = value

        def some_rows(g, carry):
            if e == 0:
                for load in piece_loads(g):
                    load.wait()
            for u in range(unroll):
                r = g * unroll + u
                line = vec[e, pl.ds(r, 1)] if e > 0 else right_ref[pl.ds(r, 1)]
                hat = jnp.sum(jac[r] * line, axis=1, keepdims=True)
                hat = jnp.broadcast_to(hat, (width, width))
                for k in range(slot_count):
                    at = pl.multiple_of(k * chunk + r * SUBLANES, SUBLANES)
                    prod[pl.ds(at, SUBLANES)] = fold(coup[r, k] * hat)
                dprod[pl.ds(pl.multiple_of(r * SUBLANES, SUBLANES), SUBLANES)] = fold(diag[r] * hat)
            return carry

        lax.fori_loop(0, rows_dev // unroll, some_rows, 0)
        rest = prod[...]
        out = None
        for _ in range(3):
            piece = rest.astype(jnp.bfloat16)
            rest = rest - piece.astype(F32)
            term = jnp.dot(one_hot[...], piece, preferred_element_type=F32)
            out = term if out is None else out + term
        landed[e] = out
        if e == 0:
            greetings = peers - 1 + (n_cols - 1) * n_sub * linked_count
            pl.semaphore_wait(barrier, greetings)
        each_route(lambda slot, step: owner_copy(e, slot, step).start())

    def own_products(e):
        at = pl.multiple_of(from_block(0, col, sub), rows_dev)
        from_at = pl.multiple_of(sub * half_rows, rows_dev)
        recv[e, pl.ds(at, rows_dev)] = landed[e, pl.ds(from_at, rows_dev)]
        return jnp.sum(dprod[...].reshape(rows_dev, SUBLANES, width), axis=1)

    def gather_products(e, own):
        await_blocks(recv_sem.at[e])
        for b in range(slots * n_cols * n_sub):
            own = own + recv[e, b * rows_dev : (b + 1) * rows_dev]
        return own

    shadow = right_ref[...]
    send_products(0, shadow)
    own = own_products(0)
    image = gather_products(0, own)

    send_products(1, image)
    dots_start(0, [shadow * shadow, shadow * image])
    own = own_products(1)
    rho, shadow_image = dots_finish(0, 2)
    alpha = rho / shadow_image
    half = shadow - alpha * image
    second = gather_products(1, own)
    twice = image - alpha * second

    send_products(2, twice)
    dots_start(1, [twice * half, twice * twice, shadow * half, shadow * twice])
    own = own_products(2)
    cross, square, shadow_half, shadow_twice = dots_finish(1, 4)
    omega = cross / square
    rho_next = shadow_half - omega * shadow_twice
    beta = rho_next / rho * (alpha / omega)
    residual = half - omega * twice
    search = residual + beta * (shadow - omega * image)
    known = twice + beta * (image - omega * second)
    third = gather_products(2, own)
    residual_image = twice - omega * third
    image = known - omega * third

    send_products(3, image)
    dots_start(2, [shadow * image])
    own = own_products(3)
    alpha_next = rho_next / dots_finish(2, 1)[0]
    half_next = residual - alpha_next * image
    fourth = gather_products(3, own)
    twice = residual_image - alpha_next * fourth
    dots_start(3, [twice * half_next, twice * twice])

    vec[0] = alpha * shadow + omega * half + alpha_next * search
    vec[1] = half_next
    at_lane = lax.broadcasted_iota(jnp.int32, (width, width), 1)

    def hats(r, carry):
        for j in range(2):
            hat = jnp.sum(jac[r] * vec[j, pl.ds(r, 1)], axis=1, keepdims=True)
            carry = jnp.where(at_lane == j * rows_dev + r, hat, carry)
        return carry

    hat = lax.fori_loop(0, rows_dev, hats, jnp.zeros((width, width), F32), unroll=4)
    hat = jnp.transpose(hat)
    for e in range(APPLIES):
        await_blocks(send_sem.at[e])
    cross, square = dots_finish(3, 2)
    omega = cross / square
    out_ref[:rows_dev] = hat[:rows_dev] + omega * hat[rows_dev : 2 * rows_dev]
    out_ref[rows_dev:] = half_next - omega * twice
    for e, count in enumerate((2, 4, 1, 2)):
        await_rows(dots_send_sem.at[e], (peers - 1) * count)


def on_device(
    diagonal_tiles, coupling_tiles, column_part, column_tile, neighbours, right_side, jacobi_inverse
):
    n_rows, n_cols, n_sub = (lax.axis_size(a) for a in ("rows", "cols", "sub"))
    slots = len(offsets_of(n_rows))
    rows_dev, slot_count, width, _ = coupling_tiles.shape
    half_rows = slots * rows_dev
    chunk = rows_dev * SUBLANES
    peers = n_rows * n_sub
    hbm = pl.BlockSpec(memory_space=pl.ANY)
    vmem = pl.BlockSpec(memory_space=pltpu.VMEM)
    dma = pltpu.SemaphoreType.DMA
    scratch = [
        pltpu.VMEM(diagonal_tiles.shape, F32),
        pltpu.VMEM(coupling_tiles.shape, F32),
        pltpu.VMEM(jacobi_inverse.shape, F32),
        pltpu.VMEM((slot_count, rows_dev), jnp.int32),
        pltpu.VMEM((slot_count, rows_dev), jnp.int32),
        pltpu.SMEM(neighbours.shape, jnp.int32),
        pltpu.VMEM(right_side.shape, F32),
        pltpu.VMEM((n_sub * half_rows, slot_count * chunk), jnp.bfloat16),
        pltpu.VMEM((slot_count * chunk, width), F32),
        pltpu.VMEM((chunk, width), F32),
        pltpu.VMEM((APPLIES, rows_dev, width), F32),
        pltpu.VMEM((APPLIES, n_sub * half_rows, width), F32),
        pltpu.VMEM((APPLIES, slots * n_cols * n_sub * rows_dev, width), F32),
        pltpu.VMEM((APPLIES, SUBLANES, width), F32),
        pltpu.VMEM((APPLIES, peers, SUBLANES, width), F32),
        dma((5 + 2 * (rows_dev // pieces_of(rows_dev)),)),
        dma((APPLIES,)),
        dma((APPLIES,)),
        dma((APPLIES,)),
        dma((APPLIES,)),
    ]
    both = pl.pallas_call(
        functools.partial(kernel, (n_rows, n_cols, n_sub)),
        out_shape=pltpu.VMEM((2 * rows_dev, width), F32),
        in_specs=[hbm] * 7,
        out_specs=vmem,
        scratch_shapes=scratch,
        compiler_params=pltpu.CompilerParams(
            collective_id=0, has_side_effects=True, vmem_limit_bytes=56 * 2**20
        ),
        name="solve",
    )(
        diagonal_tiles,
        coupling_tiles,
        jacobi_inverse,
        column_part.T,
        column_tile.T,
        neighbours,
        right_side,
    )
    return both[:rows_dev], both[rows_dev:]


def solution(mesh):
    in_specs = (
        P(("groups", "rows", "sub"), None, None),
        P(("groups", "rows", "sub"), "cols", None, None),
        P(("groups", "rows", "sub"), "cols"),
        P(("groups", "rows", "sub"), "cols"),
        P("groups", None),
        P(("groups", "rows", "sub"), None),
        P(("groups", "rows", "sub"), None, None),
    )
    out_specs = (P(("groups", "rows", "sub"), None), P(("groups", "rows", "sub"), None))
    return jax.shard_map(
        on_device, mesh=mesh, in_specs=in_specs, out_specs=out_specs, check_vma=False
    )
```

time: 34.5 us -> 31 us (0.90)
  Pallas kernels: 33.6 us -> 29.6 us
  local copies, waits for them, and re-layouts: 0 us -> 0.61 us
    pallas_call x1, Pallas kernels: 32.3 us -> 29.6 us  [on_device(): pl.pallas_call(functools.partial(kernel, (n_rows, n_cols, n_sub)), out_sh...]
    pallas_call x1 -> x0, Pallas kernels: 1.32 us -> none  [on_device(): pl.pallas_call(split, out_shape=(out, out), in_specs=[vmem], out_specs=(v...]
    slice x0 -> x1, local copies, waits for them, and re-layouts: none -> 0.61 us  [on_device(): return (both[:rows_dev], both[rows_dev:])]
where the time goes in v1:
time: 31 us; the launch traced here: 30.8 us
  Pallas kernels  29.6 us (95%)
  between operations  0.64 us (2%)
  local copies, waits for them, and re-layouts  0.61 us (2%)
    pallas_call x1, Pallas kernels, on_device(): pl.pallas_call(functools.partial(kernel, (n_rows, n_cols, n_sub)), out_sh...  29.6 us

profile of v1, /device:TPU:0, one launch (start us, length us, event | category | flops | bytes accessed | tf_op | source)
XLA Modules:
  0.0 30.8 jit_solution(16520125974053894015)
XLA Ops:
  0.6 29.6 %solve.1 = f32[32,128]{1,0:T(8,128)S(1)} custom-call(f32[16,128,128]{2,1,0:T(8,128)} %diag_hbm.1, f32[16,3,128,128]{3,2,1,0:T(8,128)} %coup_hbm.1, f32[16,128,128]{2,1,0:T(8,128)} %jac_hbm.1, s32[3,16]{1,0:T(4,128)} %bitcast.2, s32[3,16]{1,0:T(4,128)} %bitcast.3, s32[4,4]{1,0:T(4,128)} %near_hbm.1, f32[16,128]{1,0:T(8,128)} %right_hbm.1), custom_call_target="tpu_custom_call" | custom-call | tf_op jit(solution)/shard_map/solve/pallas_call | solution.py:382
  30.2 0.6 %fusion = (f32[16,128]{1,0:T(8,128)}, f32[16,128]{1,0:T(8,128)}) fusion(f32[32,128]{1,0:T(8,128)S(1)} %solve.1), kind=kLoop, calls=%fused_computation | loop fusion | bytes 32768 | tf_op jit(solution)/shard_map/slice | solution.py:401

commit v2 on v1

--- a/solution.py
+++ b/solution.py
@@ -241,9 +241,11 @@
     def fold(product):
         return jnp.sum(product.reshape(width // SUBLANES, SUBLANES, width), axis=0)
 
-    def send_products(e, value):
+    def send_products(e, value, products=()):
         if e > 0:
             vec[e] = value
+        if products:
+            dots_start(e - 1, products)
 
         def some_rows(g, carry):
             if e == 0:
@@ -291,8 +293,7 @@
     own = own_products(0)
     image = gather_products(0, own)
 
-    send_products(1, image)
-    dots_start(0, [shadow * shadow, shadow * image])
+    send_products(1, image, [shadow * shadow, shadow * image])
     own = own_products(1)
     rho, shadow_image = dots_finish(0, 2)
     alpha = rho / shadow_image
@@ -300,8 +301,7 @@
     second = gather_products(1, own)
     twice = image - alpha * second
 
-    send_products(2, twice)
-    dots_start(1, [twice * half, twice * twice, shadow * half, shadow * twice])
+    send_products(2, twice, [twice * half, twice * twice, shadow * half, shadow * twice])
     own = own_products(2)
     cross, square, shadow_half, shadow_twice = dots_finish(1, 4)
     omega = cross / square
@@ -314,8 +314,7 @@
     residual_image = twice - omega * third
     image = known - omega * third
 
-    send_products(3, image)
-    dots_start(2, [shadow * image])
+    send_products(3, image, [shadow * image])
     own = own_products(3)
     alpha_next = rho_next / dots_finish(2, 1)[0]
     half_next = residual - alpha_next * image

time: 31 us -> 29.8 us (0.961)
  Pallas kernels: 29.6 us -> 28.4 us
    pallas_call x1, Pallas kernels: 29.6 us -> 28.4 us  [on_device(): pl.pallas_call(functools.partial(kernel, (n_rows, n_cols, n_sub)), out_sh...]
where the time goes in v2:
time: 29.8 us; the launch traced here: 29.6 us
  Pallas kernels  28.4 us (95%)
  between operations  0.64 us (2%)
  local copies, waits for them, and re-layouts  0.61 us (2%)
    pallas_call x1, Pallas kernels, on_device(): pl.pallas_call(functools.partial(kernel, (n_rows, n_cols, n_sub)), out_sh...  28.4 us
    slice x1, local copies, waits for them, and re-layouts, on_device(): return (both[:rows_dev], both[rows_dev:])  0.61 us

profile of v2, /device:TPU:0, one launch (start us, length us, event | category | flops | bytes accessed | tf_op | source)
XLA Modules:
  0.0 29.6 jit_solution(4611245640987296907)
XLA Ops:
  0.6 28.4 %solve.1 = f32[32,128]{1,0:T(8,128)S(1)} custom-call(f32[16,128,128]{2,1,0:T(8,128)} %diag_hbm.1, f32[16,3,128,128]{3,2,1,0:T(8,128)} %coup_hbm.1, f32[16,128,128]{2,1,0:T(8,128)} %jac_hbm.1, s32[3,16]{1,0:T(4,128)} %bitcast.2, s32[3,16]{1,0:T(4,128)} %bitcast.3, s32[4,4]{1,0:T(4,128)} %near_hbm.1, f32[16,128]{1,0:T(8,128)} %right_hbm.1), custom_call_target="tpu_custom_call" | custom-call | tf_op jit(solution)/shard_map/solve/pallas_call | solution.py:381
  29.0 0.6 %fusion = (f32[16,128]{1,0:T(8,128)}, f32[16,128]{1,0:T(8,128)}) fusion(f32[32,128]{1,0:T(8,128)S(1)} %solve.1), kind=kLoop, calls=%fused_computation | loop fusion | bytes 32768 | tf_op jit(solution)/shard_map/slice | solution.py:400

commit v3 on v2

--- a/solution.py
+++ b/solution.py
@@ -47,6 +47,9 @@
     vec,
     landed,
     recv,
+    hub_recv,
+    kept,
+    ends,
     dots,
     dots_recv,
     load_sem,
@@ -54,14 +57,17 @@
     recv_sem,
     dots_send_sem,
     dots_recv_sem,
+    core_sem,
 ):
     n_rows, n_cols, n_sub = sizes
     offsets = offsets_of(n_rows)
     slots = len(offsets)
     rows_dev, slot_count, width, _ = coup.shape
-    half_rows = slots * rows_dev
+    part_rows = n_sub * rows_dev
     chunk = rows_dev * SUBLANES
     peers = n_rows * n_sub
+    hub = n_sub - 1
+    last = APPLIES - 1
     unroll = pieces_of(rows_dev)
     row = lax.axis_index("rows")
     col = lax.axis_index("cols")
@@ -135,8 +141,11 @@
     per_slot = n_cols * n_sub * rows_dev
     for slot in maybe:
         at = pl.ds(slot * per_slot, per_slot)
-        for e in range(APPLIES):
+        for e in range(last):
             recv[e, at] = jnp.zeros((per_slot, width), F32)
+        hub_recv[slot * per_slot * n_sub : (slot + 1) * per_slot * n_sub] = jnp.zeros(
+            (per_slot * n_sub, width), F32
+        )
 
     far_first = sorted(range(slots), key=lambda s: -min(offsets[s], n_rows - offsets[s]))
     for slot in far_first:
@@ -162,9 +171,7 @@
     place = jnp.zeros(part.shape, jnp.int32)
     for slot in range(1, slots):
         place = jnp.where(apart == offsets[slot], slot, place)
-    landing = place * rows_dev + tile
-    for j in range(1, n_sub):
-        landing = jnp.where(tile >= j * rows_dev, landing + (half_rows - rows_dev), landing)
+    landing = place * part_rows + tile
     from_row = lax.broadcasted_iota(jnp.int32, (rows_dev, chunk), 0)
     to_lane = lax.broadcasted_iota(jnp.int32, (rows_dev, chunk), 1)
     first = from_row * SUBLANES
@@ -172,7 +179,7 @@
     spread_landing = jnp.dot(
         landing.astype(F32), spread, precision=lax.Precision.HIGHEST, preferred_element_type=F32
     )
-    at_row = lax.broadcasted_iota(jnp.int32, (n_sub * half_rows, chunk), 0).astype(F32)
+    at_row = lax.broadcasted_iota(jnp.int32, (slots * part_rows, chunk), 0).astype(F32)
     for k in range(slot_count):
         hit = (spread_landing[k : k + 1] == at_row).astype(F32)
         one_hot[:, k * chunk : (k + 1) * chunk] = hit.astype(jnp.bfloat16)
@@ -188,7 +195,7 @@
     def owner_copy(e, slot, step):
         back = offsets.index(-offsets[slot] % n_rows)
         where = corner(slot, step)
-        at = pl.multiple_of(where["sub"] * half_rows + slot * rows_dev, rows_dev)
+        at = pl.multiple_of(slot * part_rows + where["sub"] * rows_dev, rows_dev)
         to = pl.multiple_of(from_block(back, col, sub), rows_dev)
         return pltpu.make_async_remote_copy(
             src_ref=landed.at[e, pl.ds(at, rows_dev)],
@@ -205,8 +212,40 @@
         for slot, step in routes:
             if_linked(slot, functools.partial(act, slot, step))
 
+    def hub_copy(slot, across):
+        back = offsets.index(-offsets[slot] % n_rows)
+        to = pl.multiple_of(from_block(back, col, sub) * n_sub, part_rows)
+        return pltpu.make_async_remote_copy(
+            src_ref=landed.at[last, pl.ds(slot * part_rows, part_rows)],
+            dst_ref=hub_recv.at[pl.ds(to, part_rows)],
+            send_sem=send_sem.at[last],
+            recv_sem=recv_sem.at[last],
+            device_id={
+                "rows": partner(slot),
+                "cols": lax.rem(col + across, n_cols),
+                "sub": jnp.int32(hub),
+            },
+            device_id_type=MESH,
+        )
+
+    def core_copy(ref, index, to, which):
+        return pltpu.make_async_remote_copy(
+            src_ref=ref.at[index],
+            dst_ref=ref.at[index],
+            send_sem=core_sem.at[2 * which],
+            recv_sem=core_sem.at[2 * which + 1],
+            device_id={"rows": row, "cols": col, "sub": jnp.int32(to)},
+            device_id_type=MESH,
+        )
+
+    def at_hub(act):
+        pl.when(sub == hub)(act)
+
+    def off_hub(act):
+        pl.when(sub != hub)(act)
+
     def await_rows(sem, count):
-        some = recv.at[0, pl.ds(0, count)]
+        some = hub_recv.at[pl.ds(0, count)]
         pltpu.make_async_copy(some, some, sem).wait()
 
     def await_blocks(sem):
@@ -271,6 +310,19 @@
             term = jnp.dot(one_hot[...], piece, preferred_element_type=F32)
             out = term if out is None else out + term
         landed[e] = out
+        if e == last:
+            at = pl.multiple_of(sub * rows_dev, rows_dev)
+            own = jnp.sum(dprod[...].reshape(rows_dev, SUBLANES, width), axis=1)
+            own = jnp.where(col == 0, own, 0.0)
+            landed[e, pl.ds(at, rows_dev)] = landed[e, pl.ds(at, rows_dev)] + own
+            for slot in far_first:
+                for across in reversed(range(n_cols)):
+                    send = functools.partial(lambda s, a: hub_copy(s, a).start(), slot, across)
+                    if (slot, across) == (0, 0):
+                        off_hub(send)
+                    else:
+                        if_linked(slot, send)
+            return
         if e == 0:
             greetings = peers - 1 + (n_cols - 1) * n_sub * linked_count
             pl.semaphore_wait(barrier, greetings)
@@ -278,7 +330,7 @@
 
     def own_products(e):
         at = pl.multiple_of(from_block(0, col, sub), rows_dev)
-        from_at = pl.multiple_of(sub * half_rows, rows_dev)
+        from_at = pl.multiple_of(sub * rows_dev, rows_dev)
         recv[e, pl.ds(at, rows_dev)] = landed[e, pl.ds(from_at, rows_dev)]
         return jnp.sum(dprod[...].reshape(rows_dev, SUBLANES, width), axis=1)
 
@@ -313,14 +365,44 @@
     third = gather_products(2, own)
     residual_image = twice - omega * third
     image = known - omega * third
+    kept[sub, 0] = residual_image
+    kept[sub, 1] = residual
+    kept[sub, 2] = image
+
+    @off_hub
+    def _():
+        core_copy(kept, sub, hub, 0).start()
 
     send_products(3, image, [shadow * image])
-    own = own_products(3)
     alpha_next = rho_next / dots_finish(2, 1)[0]
     half_next = residual - alpha_next * image
-    fourth = gather_products(3, own)
-    twice = residual_image - alpha_next * fourth
-    dots_start(3, [twice * half_next, twice * twice])
+
+    @at_hub
+    def _():
+        at = pl.multiple_of(from_block(0, col, sub) * n_sub, part_rows)
+        hub_recv[pl.ds(at, part_rows)] = landed[last, :part_rows]
+        if n_sub > 1:
+            await_rows(core_sem.at[1], (n_sub - 1) * 3 * rows_dev)
+        for_linked_count(
+            lambda total: await_rows(recv_sem.at[last], (total * n_cols * n_sub - 1) * part_rows)
+        )
+        fourth = hub_recv[:part_rows]
+        for b in range(1, slots * n_cols * n_sub):
+            fourth = fourth + hub_recv[b * part_rows : (b + 1) * part_rows]
+        cross = jnp.zeros((rows_dev, width), F32)
+        square = jnp.zeros((rows_dev, width), F32)
+        for t in range(n_sub):
+            end = kept[t, 0] - alpha_next * fourth[t * rows_dev : (t + 1) * rows_dev]
+            cross = cross + end * (kept[t, 1] - alpha_next * kept[t, 2])
+            square = square + end * end
+            ends[t] = end
+        for j, product in enumerate((cross, square)):
+            dots[last, j : j + 1] = jnp.sum(product, axis=0, keepdims=True)
+        for _, where in dot_peers():
+            dots_copy(last, 2, where).start()
+        for t in range(hub):
+            core_copy(ends, t, t, 1).start()
+        dots_recv[last, me, :2] = dots[last, :2]
 
     vec[0] = alpha * shadow + omega * half + alpha_next * search
     vec[1] = half_next
@@ -334,14 +416,35 @@
 
     hat = lax.fori_loop(0, rows_dev, hats, jnp.zeros((width, width), F32), unroll=4)
     hat = jnp.transpose(hat)
-    for e in range(APPLIES):
+    for e in range(last):
         await_blocks(send_sem.at[e])
-    cross, square = dots_finish(3, 2)
-    omega = cross / square
+    for e, count in enumerate((2, 4, 1)):
+        await_rows(dots_send_sem.at[e], (peers - 1) * count)
+
+    @at_hub
+    def _():
+        for_linked_count(
+            lambda total: await_rows(send_sem.at[last], (total * n_cols - 1) * part_rows)
+        )
+        await_rows(dots_send_sem.at[last], (peers - 1) * 2)
+        if hub > 0:
+            await_rows(core_sem.at[2], hub * rows_dev)
+        await_rows(dots_recv_sem.at[last], (n_rows - 1) * 2)
+
+    @off_hub
+    def _():
+        for_linked_count(lambda total: await_rows(send_sem.at[last], total * n_cols * part_rows))
+        await_rows(core_sem.at[0], 3 * rows_dev)
+        await_rows(core_sem.at[3], rows_dev)
+        await_rows(dots_recv_sem.at[last], n_rows * 2)
+
+    lines = dots_recv[last, hub, :2]
+    for r in range(1, n_rows):
+        lines = lines + dots_recv[last, r * n_sub + hub, :2]
+    total = jnp.sum(lines, axis=1, keepdims=True)
+    omega = jnp.broadcast_to(total[:1], (1, width)) / jnp.broadcast_to(total[1:], (1, width))
     out_ref[:rows_dev] = hat[:rows_dev] + omega * hat[rows_dev : 2 * rows_dev]
-    out_ref[rows_dev:] = half_next - omega * twice
-    for e, count in enumerate((2, 4, 1, 2)):
-        await_rows(dots_send_sem.at[e], (peers - 1) * count)
+    out_ref[rows_dev:] = half_next - omega * ends[sub]
 
 
 def on_device(
@@ -350,7 +453,7 @@
     n_rows, n_cols, n_sub = (lax.axis_size(a) for a in ("rows", "cols", "sub"))
     slots = len(offsets_of(n_rows))
     rows_dev, slot_count, width, _ = coupling_tiles.shape
-    half_rows = slots * rows_dev
+    part_rows = n_sub * rows_dev
     chunk = rows_dev * SUBLANES
     peers = n_rows * n_sub
     hbm = pl.BlockSpec(memory_space=pl.ANY)
@@ -364,12 +467,15 @@
         pltpu.VMEM((slot_count, rows_dev), jnp.int32),
         pltpu.SMEM(neighbours.shape, jnp.int32),
         pltpu.VMEM(right_side.shape, F32),
-        pltpu.VMEM((n_sub * half_rows, slot_count * chunk), jnp.bfloat16),
+        pltpu.VMEM((slots * part_rows, slot_count * chunk), jnp.bfloat16),
         pltpu.VMEM((slot_count * chunk, width), F32),
         pltpu.VMEM((chunk, width), F32),
         pltpu.VMEM((APPLIES, rows_dev, width), F32),
-        pltpu.VMEM((APPLIES, n_sub * half_rows, width), F32),
-        pltpu.VMEM((APPLIES, slots * n_cols * n_sub * rows_dev, width), F32),
+        pltpu.VMEM((APPLIES, slots * part_rows, width), F32),
+        pltpu.VMEM((APPLIES - 1, slots * n_cols * part_rows, width), F32),
+        pltpu.VMEM((slots * n_cols * n_sub * part_rows, width), F32),
+        pltpu.VMEM((n_sub, 3, rows_dev, width), F32),
+        pltpu.VMEM((n_sub, rows_dev, width), F32),
         pltpu.VMEM((APPLIES, SUBLANES, width), F32),
         pltpu.VMEM((APPLIES, peers, SUBLANES, width), F32),
         dma((5 + 2 * (rows_dev // pieces_of(rows_dev)),)),
@@ -377,6 +483,7 @@
         dma((APPLIES,)),
         dma((APPLIES,)),
         dma((APPLIES,)),
+        dma((4,)),
     ]
     both = pl.pallas_call(
         functools.partial(kernel, (n_rows, n_cols, n_sub)),

time: 29.8 us -> 28.9 us (0.970)
  Pallas kernels: 28.4 us -> 27.5 us
    pallas_call x1, Pallas kernels: 28.4 us -> 27.5 us  [on_device(): pl.pallas_call(functools.partial(kernel, (n_rows, n_cols, n_sub)), out_sh...]
where the time goes in v3:
time: 28.9 us; the launch traced here: 28.8 us
  Pallas kernels  27.5 us (95%)
  between operations  0.64 us (2%)
  local copies, waits for them, and re-layouts  0.61 us (2%)
    pallas_call x1, Pallas kernels, on_device(): pl.pallas_call(functools.partial(kernel, (n_rows, n_cols, n_sub)), out_sh...  27.5 us
    slice x1, local copies, waits for them, and re-layouts, on_device(): return (both[:rows_dev], both[rows_dev:])  0.61 us

profile of v3, /device:TPU:0, one launch (start us, length us, event | category | flops | bytes accessed | tf_op | source)
XLA Modules:
  0.0 28.8 jit_solution(3807273937255254115)
XLA Ops:
  0.6 27.5 %solve.1 = f32[32,128]{1,0:T(8,128)S(1)} custom-call(f32[16,128,128]{2,1,0:T(8,128)} %diag_hbm.1, f32[16,3,128,128]{3,2,1,0:T(8,128)} %coup_hbm.1, f32[16,128,128]{2,1,0:T(8,128)} %jac_hbm.1, s32[3,16]{1,0:T(4,128)} %bitcast.2, s32[3,16]{1,0:T(4,128)} %bitcast.3, s32[4,4]{1,0:T(4,128)} %near_hbm.1, f32[16,128]{1,0:T(8,128)} %right_hbm.1), custom_call_target="tpu_custom_call" | custom-call | tf_op jit(solution)/shard_map/solve/pallas_call | solution.py:488
  28.2 0.6 %fusion = (f32[16,128]{1,0:T(8,128)}, f32[16,128]{1,0:T(8,128)}) fusion(f32[32,128]{1,0:T(8,128)S(1)} %solve.1), kind=kLoop, calls=%fused_computation | loop fusion | bytes 32768 | tf_op jit(solution)/shard_map/slice | solution.py:507

commit v4 on v3

--- a/solution.py
+++ b/solution.py
@@ -304,7 +304,7 @@
         lax.fori_loop(0, rows_dev // unroll, some_rows, 0)
         rest = prod[...]
         out = None
-        for _ in range(3):
+        for _ in range(2):
             piece = rest.astype(jnp.bfloat16)
             rest = rest - piece.astype(F32)
             term = jnp.dot(one_hot[...], piece, preferred_element_type=F32)

time: 28.9 us -> 28.8 us (level)
  no operation moved by 1% of the time
where the time goes in v4:
time: 28.8 us; the launch traced here: 28.6 us
  Pallas kernels  27.4 us (95%)
  between operations  0.64 us (2%)
  local copies, waits for them, and re-layouts  0.61 us (2%)
    pallas_call x1, Pallas kernels, on_device(): pl.pallas_call(functools.partial(kernel, (n_rows, n_cols, n_sub)), out_sh...  27.4 us
    slice x1, local copies, waits for them, and re-layouts, on_device(): return (both[:rows_dev], both[rows_dev:])  0.61 us

profile of v4, /device:TPU:0, one launch (start us, length us, event | category | flops | bytes accessed | tf_op | source)
XLA Modules:
  0.0 28.6 jit_solution(16284967363522491502)
XLA Ops:
  0.6 27.4 %solve.1 = f32[32,128]{1,0:T(8,128)S(1)} custom-call(f32[16,128,128]{2,1,0:T(8,128)} %diag_hbm.1, f32[16,3,128,128]{3,2,1,0:T(8,128)} %coup_hbm.1, f32[16,128,128]{2,1,0:T(8,128)} %jac_hbm.1, s32[3,16]{1,0:T(4,128)} %bitcast.2, s32[3,16]{1,0:T(4,128)} %bitcast.3, s32[4,4]{1,0:T(4,128)} %near_hbm.1, f32[16,128]{1,0:T(8,128)} %right_hbm.1), custom_call_target="tpu_custom_call" | custom-call | tf_op jit(solution)/shard_map/solve/pallas_call | solution.py:488
  28.0 0.6 %fusion = (f32[16,128]{1,0:T(8,128)}, f32[16,128]{1,0:T(8,128)}) fusion(f32[32,128]{1,0:T(8,128)S(1)} %solve.1), kind=kLoop, calls=%fused_computation | loop fusion | bytes 32768 | tf_op jit(solution)/shard_map/slice | solution.py:507

commit v5 on v4

--- a/solution.py
+++ b/solution.py
@@ -76,10 +76,12 @@
 
     def piece_loads(g):
         at = pl.ds(g * unroll, unroll)
-        return [
-            pltpu.make_async_copy(diag_hbm.at[at], diag.at[at], load_sem.at[5 + 2 * g]),
-            pltpu.make_async_copy(coup_hbm.at[at], coup.at[at], load_sem.at[6 + 2 * g]),
-        ]
+        first_sem = 5 + (1 + slot_count) * g
+        loads = [pltpu.make_async_copy(diag_hbm.at[at], diag.at[at], load_sem.at[first_sem])]
+        for k in range(slot_count):
+            sem = load_sem.at[first_sem + 1 + k]
+            loads.append(pltpu.make_async_copy(coup_hbm.at[at, k], coup.at[at, k], sem))
+        return loads
 
     small = [
         pltpu.make_async_copy(part_hbm, part_ref, load_sem.at[0]),
@@ -478,7 +480,7 @@
         pltpu.VMEM((n_sub, rows_dev, width), F32),
         pltpu.VMEM((APPLIES, SUBLANES, width), F32),
         pltpu.VMEM((APPLIES, peers, SUBLANES, width), F32),
-        dma((5 + 2 * (rows_dev // pieces_of(rows_dev)),)),
+        dma((5 + (1 + slot_count) * (rows_dev // pieces_of(rows_dev)),)),
         dma((APPLIES,)),
         dma((APPLIES,)),
         dma((APPLIES,)),

time: 28.8 us -> 28.8 us (level)
  no operation moved by 1% of the time
where the time goes in v5:
time: 28.8 us; the launch traced here: 28.6 us
  Pallas kernels  27.4 us (95%)
  between operations  0.64 us (2%)
  local copies, waits for them, and re-layouts  0.61 us (2%)
    pallas_call x1, Pallas kernels, on_device(): pl.pallas_call(functools.partial(kernel, (n_rows, n_cols, n_sub)), out_sh...  27.4 us
    slice x1, local copies, waits for them, and re-layouts, on_device(): return (both[:rows_dev], both[rows_dev:])  0.61 us

profile of v5, /device:TPU:0, one launch (start us, length us, event | category | flops | bytes accessed | tf_op | source)
XLA Modules:
  0.0 28.6 jit_solution(9067409551545886435)
XLA Ops:
  0.6 27.4 %solve.1 = f32[32,128]{1,0:T(8,128)S(1)} custom-call(f32[16,128,128]{2,1,0:T(8,128)} %diag_hbm.1, f32[16,3,128,128]{3,2,1,0:T(8,128)} %coup_hbm.1, f32[16,128,128]{2,1,0:T(8,128)} %jac_hbm.1, s32[3,16]{1,0:T(4,128)} %bitcast.2, s32[3,16]{1,0:T(4,128)} %bitcast.3, s32[4,4]{1,0:T(4,128)} %near_hbm.1, f32[16,128]{1,0:T(8,128)} %right_hbm.1), custom_call_target="tpu_custom_call" | custom-call | tf_op jit(solution)/shard_map/solve/pallas_call | solution.py:490
  28.0 0.6 %fusion = (f32[16,128]{1,0:T(8,128)}, f32[16,128]{1,0:T(8,128)}) fusion(f32[32,128]{1,0:T(8,128)S(1)} %solve.1), kind=kLoop, calls=%fused_computation | loop fusion | bytes 32768 | tf_op jit(solution)/shard_map/slice | solution.py:509
